TPU v7x, 32 devices: a whole 2x2x4 slice. The times are simulated.
32 devices in a mesh: cuts: 4 (over z), dev: 8 (over y, x, core).
Axes of the slice: x: 2, y: 2, z: 4, core: 2. Of those that a mesh axis runs over, the one named last changes fastest.
Arguments:
- inputs: bfloat16 [16384, 3072], P(('cuts', 'dev')), may hold values from -6 to 6
- cotangent: bfloat16 [16384, 512], P(('cuts', 'dev')), may hold values from -0.29882812 to 0.29882812
- errors: bfloat16 [32, 3072, 512], P(('cuts', 'dev')), may hold values from -6 to 6
- previous_q: float32 [512, 64], replicated, may hold values from -0.25 to 0.25
Outputs:
- new_errors: bfloat16 [32, 3072, 512], P(('cuts', 'dev'))
- p_hat: float32 [3072, 64], replicated
- q_mean: float32 [512, 64], replicated
All inputs are finite; a program needn't handle non-finite values.
Results may differ from a plain program's by a relative error of at most 0.001.
Values sent between devices are 32-bit elements; how exact they have to be, the bound alone decides.
No kernel may reach another device: no remote copies, remote signals or barrier semaphores. Data moves between devices by JAX's collectives and lax.ppermute only.
A program may use at most 64 MiB of HBM per device.

v0:
```python
import functools

import jax
import jax.numpy as jnp
from jax import lax
from jax.experimental import pallas as pl
from jax.experimental.pallas import tpu as pltpu
from jax.sharding import Mesh, PartitionSpec as P


F32 = jnp.float32
BF16 = jnp.bfloat16
LANES = 128
VM = pl.BlockSpec(memory_space=pltpu.VMEM)
HBM = pl.BlockSpec(memory_space=pltpu.HBM)
SM = pl.BlockSpec(memory_space=pltpu.SMEM)
NN = (((1,), (0,)), ((), ()))
NT = (((1,), (1,)), ((), ()))
TN = (((0,), (0,)), ((), ()))


def dot(a, b, dims, precision=None):
    return lax.dot_general(a, b, dims, precision=precision, preferred_element_type=F32)


def split3(x):
    high = x.astype(BF16)
    rest = x - high.astype(F32)
    mid = rest.astype(BF16)
    low = (rest - mid.astype(F32)).astype(BF16)
    return jnp.concatenate([high, mid, low], axis=0)


def fold3(x):
    rows = x.shape[0] // 3
    return x[:rows] + x[rows : 2 * rows] + x[2 * rows :]


def call(kernel, outs, ins_specs, out_specs, scratch, args, flops, limit, aliases={}):
    return pl.pallas_call(
        kernel,
        out_shape=outs,
        in_specs=ins_specs,
        out_specs=out_specs,
        scratch_shapes=scratch,
        compiler_params=pltpu.CompilerParams(vmem_limit_bytes=limit * 1024 * 1024),
        cost_estimate=pl.CostEstimate(flops=flops, bytes_accessed=0, transcendentals=0),
        input_output_aliases=aliases,
    )(*args)


def vmem(shape, dtype=F32):
    return jax.ShapeDtypeStruct(shape, dtype)


def left_half(total, block, start, xv, ev, v3, q3):
    rank = v3.shape[0] // 3
    for i in range(total.shape[0] // rank * LANES // block):
        cut = pl.ds(pl.multiple_of(start + i * block, LANES), block)
        part = fold3(dot(v3[...], xv[:, cut], NN) + dot(q3[...], ev[cut, :], NT))
        for j in range(block // LANES):
            at = (i * (block // LANES) + j) * rank
            total[at : at + rank, :] = part[:, j * LANES : (j + 1) * LANES]


def put_chips(chips, ids, total, out):
    size = out.shape[0] // chips
    for chip in range(chips):
        start = pl.multiple_of((chip ^ ids[1]) * size, 8)
        out[chip * size : (chip + 1) * size, :] = total[pl.ds(start, size), :]


def cuts_of(block, start, half):
    return [pl.ds(pl.multiple_of(start + i * block, LANES), block) for i in range(half // block)]


def load_kernel(cores, block, ids, e_hbm, ev, sem):
    half = ev.shape[0] // cores
    cut = cuts_of(block, (1 - ids[0]) * half, half)[0]
    copy = pltpu.make_async_copy(e_hbm.at[0, cut, :], ev.at[cut, :], sem)
    copy.start()
    copy.wait()


def first_kernel(cores, chips, block, ids, x_hbm, e_hbm, y, q, e_in, send, xv, ev, v3, q3, total, sem):
    half = xv.shape[1] // cores
    theirs, own = cuts_of(block, (1 - ids[0]) * half, half), cuts_of(block, ids[0] * half, half)
    count = len(own)
    x_copies, e_copies = [], []
    for i, cut in enumerate(theirs + own):
        x_copies.append(pltpu.make_async_copy(x_hbm.at[:, cut], xv.at[:, cut], sem.at[2 * i]))
        if i > 0:
            e_copies.append(pltpu.make_async_copy(e_hbm.at[0, cut, :], ev.at[cut, :], sem.at[2 * i + 1]))
    for copy in e_copies[: count - 1] + x_copies + e_copies[count - 1 :]:
        copy.start()
    q3[...] = split3(q[...])
    rank = q.shape[0]
    tiles = block // LANES
    for i, cut in enumerate(theirs):
        if i > 0:
            e_copies[i - 1].wait()
        part = fold3(dot(q3[...], (e_in if i == 0 else ev)[cut, :], NT))
        for j in range(tiles):
            at = (i * tiles + j) * rank
            total[at : at + rank, :] = part[:, j * LANES : (j + 1) * LANES]
        if i == 0:
            v3[...] = split3(fold3(dot(q3[...], y[...], NT)))
    for i, cut in enumerate(theirs):
        x_copies[i].wait()
        part = fold3(dot(v3[...], xv[:, cut], NN))
        for j in range(tiles):
            at = (i * tiles + j) * rank
            total[at : at + rank, :] += part[:, j * LANES : (j + 1) * LANES]
    put_chips(chips, ids, total, send)
    for copy in x_copies[count:] + e_copies[count - 1 :]:
        copy.wait()


def second_kernel(chips, block, ids, xv, ev, v3, q3, keep, total):
    left_half(total, block, ids[0] * (total.shape[0] // (v3.shape[0] // 3) * LANES), xv, ev, v3, q3)
    put_chips(chips, ids, total, keep)


def sum_kernel(count, *refs):
    ins, outs = refs[:count], refs[count:]
    size = outs[0].shape[0]
    for k, out in enumerate(outs):
        rows = pl.ds(k * size, size)
        total = ins[0][rows, :]
        for other in ins[1:]:
            total = total + other[rows, :]
        out[...] = total


def add_up(ins, pieces):
    rows = ins[0].shape[0]
    shape = vmem((rows // pieces, LANES))
    return call(
        functools.partial(sum_kernel, len(ins)), [shape] * pieces, [VM] * len(ins), [VM] * pieces, [], ins, 10**7, 8
    )


def merge_kernel(span, xv, yv, ev, merged, parts):
    for i in range(ev.shape[0] // span):
        cut = slice(i * span, (i + 1) * span)
        block = dot(xv[:, cut], yv[...], TN) + ev[cut, :].astype(F32)
        merged[cut, :] = block
        high = block.astype(BF16)
        parts[2 * i * span : (2 * i + 1) * span, :] = high
        parts[(2 * i + 1) * span : (2 * i + 2) * span, :] = (block - high.astype(F32)).astype(BF16)


def chunk_of(chips, ids, where):
    return (where[0] ^ ids[0]) * chips + (where[1] ^ ids[1])


def chunk_kernel(chips, places, first, last, ids, *refs):
    parts, rest = refs[: len(places)], refs[len(places) :]
    merged2, rest = rest[0], rest[1:]
    before, rest = (None, rest) if first else (rest[0], rest[1:])
    p3 = rest[0]
    rank = p3.shape[0] // 3
    span = parts[0].shape[0] // rank * LANES
    t = None if first else before[...]
    for i, (part, where) in enumerate(zip(parts, places)):
        for c in range(span // LANES):
            at = i * span + c * LANES
            p3[:, at : at + LANES] = split3(part[c * rank : (c + 1) * rank, :])
        rows = pl.ds(pl.multiple_of(chunk_of(chips, ids, where) * (2 * span), 16), 2 * span)
        mine = p3[:, i * span : (i + 1) * span]
        new = dot(jnp.concatenate([mine, mine], axis=1), merged2[rows, :], NN)
        t = new if t is None else t + new
    if not last:
        rest[1][...] = t
        return
    keep, send, total = rest[1:]
    right = fold3(t)
    for c in range(right.shape[1] // LANES):
        total[c * rank : (c + 1) * rank, :] = right[:, c * LANES : (c + 1) * LANES]
    size = keep.shape[0]
    keep[...] = total[pl.ds(pl.multiple_of(ids[0] * size, 8), size), :]
    send[...] = total[pl.ds(pl.multiple_of((1 - ids[0]) * size, 8), size), :]


def gram_kernel(*refs):
    gram = refs[-1]
    rank = gram.shape[0]
    full = sum(dot(p3[...], p3[...], NT) for p3 in refs[:-1])
    full = fold3(full)
    gram[...] = full[:, :rank] + full[:, rank : 2 * rank] + full[:, 2 * rank :]


def factor_kernel(gram, lower_inv):
    rank = gram.shape[0]
    n = 8
    row = lax.broadcasted_iota(jnp.int32, (rank, rank), 0)
    lane = lax.broadcasted_iota(jnp.int32, (rank, rank), 1)
    eye = jnp.where(lane == row, 1.0, 0.0).astype(F32)
    work = jnp.concatenate([eye, gram[...]], axis=1)
    groups = [work[n * g : n * g + n, :] for g in range(rank // n)]
    wide = (n, 2 * rank)
    def column(x, k):
        return jnp.broadcast_to(x[:, rank + k : rank + k + 1], wide)
    def line(x, i):
        return jnp.broadcast_to(x[i : i + 1, :], wide)
    sub = lax.broadcasted_iota(jnp.int32, wide, 0)
    for g in range(rank // n):
        base = n * g
        cols = [column(groups[g], base + j) for j in range(n)]
        b = {(i, j): line(cols[j], i) for j in range(n) for i in range(j, n)}
        low, inv = {}, []
        for s in range(n):
            inv.append(1.0 / b[s, s])
            for i in range(s + 1, n):
                low[i, s] = b[i, s] * inv[s]
            for j in range(s + 1, n):
                for i in range(j, n):
                    b[i, j] = b[i, j] - low[i, s] * b[j, s]
        rows = []
        for i in range(n):
            r = line(groups[g], i)
            for s in range(i):
                r = r - low[i, s] * rows[s]
            rows.append(r)
        for h in range(g + 1, rank // n):
            x = [column(groups[h], base + s) for s in range(n)]
            for s in range(n):
                for t in range(s):
                    x[s] = x[s] - low[s, t] * x[t]
            new = groups[h]
            for s in range(n):
                new = new - (x[s] * inv[s]) * rows[s]
            groups[h] = new
        out = jnp.zeros(wide, F32)
        for i in range(n):
            out = jnp.where(sub == i, rows[i] * jnp.sqrt(inv[i]), out)
        lower_inv[base : base + n, :] = out[:, :rank]


def hat_kernel(cores, chips, places, ids, *refs):
    p3s, (lower_inv, out, hat3, p_hat, sem) = refs[:-5], refs[-5:]
    rank = lower_inv.shape[0]
    inv3 = split3(lower_inv[...])
    at = 0
    for p3 in p3s:
        full = dot(inv3, p3[:rank, :], NN)
        mids = dot(inv3[: 2 * rank], p3[rank : 2 * rank, :], NN)
        hats = fold3(full) + (mids[:rank] + mids[rank:]) + dot(inv3[:rank], p3[2 * rank :, :], NN)
        span = p_hat.shape[1] // (cores * chips)
        for i in range(p3.shape[1] // span):
            start = chunk_of(chips, ids, places[at]) * span
            at += 1
            hat = hats[:, i * span : (i + 1) * span]
            p_hat[:, pl.ds(pl.multiple_of(start, LANES), span)] = hat
            for c in range(span // LANES):
                turned = hat[:, c * LANES : (c + 1) * LANES].T
                high = turned.astype(BF16)
                low = (turned - high.astype(F32)).astype(BF16)
                rows = pl.ds(pl.multiple_of(start + c * LANES, LANES), LANES)
                hat3[rows, :] = jnp.concatenate([high, low, high], axis=1)
    copy = pltpu.make_async_copy(p_hat, out, sem)
    copy.start()
    copy.wait()


def last_kernel(devices, block, ids, keep, other, lower_inv, hat3, merged, new_errors, q_mean, total, out, q_out, sem):
    rank = lower_inv.shape[0]
    half = keep.shape[0]
    total[pl.ds(pl.multiple_of(ids[0] * half, 8), half), :] = keep[...]
    if other is not None:
        total[pl.ds(pl.multiple_of((1 - ids[0]) * half, 8), half), :] = other[...]
    wide = jnp.concatenate([total[c * rank : (c + 1) * rank, :] for c in range(total.shape[0] // rank)], axis=1)
    a, b = split3(lower_inv[...]), split3(wide)
    ah, am, al = a[:rank], a[rank : 2 * rank], a[2 * rank :]
    bh, bm, bl = b[:rank], b[rank : 2 * rank], b[2 * rank :]
    right = dot(jnp.concatenate([ah, ah, am, ah, al, am], axis=1), jnp.concatenate([bh, bm, bh, bl, bh, bm], axis=0), NN)
    right = right / devices
    high = right.astype(BF16)
    low = (right - high.astype(F32)).astype(BF16)
    q3 = jnp.concatenate([high, high, low], axis=0)
    q_out[...] = right
    copies = [pltpu.make_async_copy(q_out, q_mean, sem.at[0])]
    copies[0].start()
    for i in range(merged.shape[0] // block):
        cut = pl.ds(i * block, block)
        out[cut, :] = (merged[cut, :] - dot(hat3[cut, :], q3, NN)).astype(BF16)
        copies.append(pltpu.make_async_copy(out.at[cut, :], new_errors.at[0, cut, :], sem.at[1 + i]))
        copies[1 + i].start()
    for copy in copies:
        copy.wait()


def exchange(parts, axis, size):
    return [parts[0]] + [swap(parts[k], axis, size, k) for k in range(1, size)]


def swap(x, axis, size, by):
    return lax.ppermute(x, axis, [(i, i ^ by) for i in range(size)])


def body(sizes, *args):
    return step(sizes, *args)


def step(sizes, inputs, cotangent, errors, previous_q):
    cores, chips, groups, cuts = sizes
    tokens, depth = inputs.shape
    width, rank = previous_q.shape
    devices = cores * chips * groups * cuts
    rows = depth * rank // LANES
    span = depth // (cores * chips)
    block = next(b for b in (512, 384, 256, LANES) if depth // cores % b == 0)
    tail = block // 2
    ids = jnp.stack([lax.axis_index("core"), lax.axis_index("chip")]).astype(jnp.int32)
    half = vmem((rows // cores, LANES))
    total = pltpu.VMEM((rows // cores, LANES), F32)
    held = vmem((depth, width), BF16)
    blocks = depth // cores // block
    ev = call(
        functools.partial(load_kernel, cores, block),
        held,
        [SM, HBM],
        VM,
        [pltpu.SemaphoreType.DMA],
        (ids, errors),
        10**9,
        49,
    )
    send, xv, ev, v3, q3 = call(
        functools.partial(first_kernel, cores, chips, block),
        [half, vmem((tokens, depth), BF16), held, vmem((3 * rank, tokens), BF16), vmem((3 * rank, width), BF16)],
        [SM, HBM, HBM] + [VM] * 3,
        [VM] * 5,
        [total, pltpu.SemaphoreType.DMA((4 * blocks,))],
        (ids, inputs, errors, cotangent, previous_q.T, ev),
        10**9,
        46,
        {5: 2},
    )
    got = swap(send, "core", cores, 1)
    keep = call(
        functools.partial(second_kernel, chips, block),
        half,
        [SM] + [VM] * 4,
        VM,
        [total],
        (ids, xv, ev, v3, q3),
        10**9,
        8,
    )
    parts = add_up([keep, got], chips)
    parts = add_up(exchange(parts, "chip", chips), 1)
    if groups > 1:
        parts = add_up(exchange(parts * groups, "group", groups), 1)
    parts = add_up(exchange(parts * cuts, "cuts", cuts), 1)
    parts = exchange(parts * chips, "chip", chips)
    parts = parts + [swap(part, "core", cores, 1) for part in parts]

    merged, merged2 = call(
        functools.partial(merge_kernel, span),
        [vmem((depth, width)), vmem((2 * depth, width), BF16)],
        [VM] * 3,
        [VM] * 2,
        [],
        (xv, cotangent, ev),
        10**9,
        8,
    )
    places = [(core, chip) for core in range(cores) for chip in range(chips)]
    batches = [[0], [chips, *range(1, chips)], list(range(chips + 1, 2 * chips))]
    share = vmem((width * rank // LANES // cores, LANES))
    sums, p3s, order = [], [], []
    for at, batch in enumerate(batches):
        end = at == len(batches) - 1
        p3, *sums = call(
            functools.partial(chunk_kernel, chips, [places[k] for k in batch], at == 0, end),
            [vmem((3 * rank, span * len(batch)), BF16)] + ([share, share] if end else [vmem((3 * rank, width))]),
            [SM] + [VM] * (len(batch) + 1 + len(sums)),
            [VM] * (3 if end else 2),
            [pltpu.VMEM((width * rank // LANES, LANES), F32)] if end else [],
            (ids, *[parts[k] for k in batch], merged2, *sums),
            10**8,
            8,
        )
        p3s.append(p3)
        order += [places[k] for k in batch]
    keep, send = sums
    got = swap(send, "core", cores, 1)
    part = add_up([keep, got], 1)[0]
    part = add_up(exchange([part] * chips, "chip", chips), 1)[0]
    if groups > 1:
        part = add_up(exchange([part] * groups, "group", groups), 1)[0]
    part = add_up(exchange([part] * cuts, "cuts", cuts), 1)[0]
    other = swap(part, "core", cores, 1)

    gram = call(gram_kernel, vmem((rank, rank)), [VM] * len(p3s), VM, [], p3s, 10**8, 8)
    lower_inv = call(factor_kernel, vmem((rank, rank)), [VM], VM, [], (gram,), 10**9, 8)
    p_hat, hat3 = call(
        functools.partial(hat_kernel, cores, chips, order),
        [vmem((rank, depth)), vmem((depth, 3 * rank), BF16)],
        [SM] + [VM] * (len(p3s) + 1),
        [HBM, VM],
        [pltpu.VMEM((rank, depth), F32), pltpu.SemaphoreType.DMA],
        (ids, *p3s, lower_inv),
        10**9,
        8,
    )
    new_errors, q_mean = call(
        functools.partial(last_kernel, devices, tail),
        [vmem((1, depth, width), BF16), vmem((rank, width))],
        [SM] + [VM] * 5,
        [HBM] * 2,
        [
            pltpu.VMEM((width * rank // LANES, LANES), F32),
            pltpu.VMEM((depth, width), BF16),
            pltpu.VMEM((rank, width), F32),
            pltpu.SemaphoreType.DMA((1 + depth // tail,)),
        ],
        (ids, part, other, lower_inv, hat3, merged),
        10**9,
        16,
    )
    return (new_errors, p_hat.T, q_mean.T)


def solution(mesh):
    cuts, dev = mesh.shape["cuts"], mesh.shape["dev"]
    cores = 2
    every = ("cuts", "group", "chip", "core")

    def program(inputs, cotangent, errors, previous_q):
        columns = inputs.shape[1] // (cores * LANES)
        chips = next(n for n in range(dev // cores, 0, -1) if dev // cores % n == 0 and columns % n == 0)
        groups = dev // (cores * chips)
        fine = Mesh(mesh.devices.reshape(cuts, groups, chips, cores), every)
        run = jax.shard_map(
            functools.partial(body, (cores, chips, groups, cuts)),
            mesh=fine,
            in_specs=(P(every, None), P(every, None), P(every, None, None), P()),
            out_specs=(P(every, None, None), P(), P()),
            check_vma=False,
        )
        return run(inputs, cotangent, errors, previous_q)

    return program
```

profile of v0, /device:TPU:0, one launch (start us, length us, event | category | flops | bytes accessed | tf_op | source)
XLA Modules:
  0.0 65.5 jit_solution(447300960635175504)
XLA Ops:
  0.7 1.6 %shard_map.67.e_in = bf16[3072,512]{1,0:T(8,128)(2,1)S(1)} custom-call(s32[2]{0:T(128)S(1)} %pad_add_fusion.ids, bf16[1,3072,512]{2,1,0:T(8,128)(2,1)} %e_hbm.3), custom_call_target="tpu_custom_call" | custom-call | flops 1000000000 | tf_op jit(solution)/shard_map/pallas_call | solution.py:40
  2.3 3.3 %shard_map.68 = (f32[768,128]{1,0:T(8,128)S(1)}, bf16[512,3072]{1,0:T(8,128)(2,1)S(1)}, bf16[3072,512]{1,0:T(8,128)(2,1)S(1)}, bf16[192,512]{1,0:T(8,128)(2,1)S(1)}, bf16[192,512]{1,0:T(8,128)(2,1)S(1)}) custom-call(s32[2]{0:T(128)S(1)} %pad_add_fusion.ids, bf16[512,3072]{1,0:T(8,128)(2,1)} %x_hbm.1, ...), custom_call_target="tpu_custom_call", output_to_operand_aliasing={{2}: (5, {})} | custom-call | flops 1000000000 | tf_op jit(solution)/shard_map/pallas_call | solution.py:40
  6.2 1.5 %shard_map.69.refs_0_ = f32[768,128]{1,0:T(8,128)S(1)} custom-call(s32[2]{0:T(128)S(1)} %pad_add_fusion.ids, bf16[512,3072]{1,0:T(8,128)(2,1)S(1)} %get-tuple-element.25.xv, bf16[3072,512]{1,0:T(8,128)(2,1)S(1)} %get-tuple-element.26.ev, bf16[192,512]{1,0:T(8,128)(2,1)S(1)} %get-tuple-element.27.v3, bf16[192,512]{1,0:T(8,128)(2,1)S(1)} %get-tuple-element.28.q3), custom_call_target="tpu_custom_call" | custom-call | flops 1000000000 | tf_op jit(solution)/shard_map/pallas_call | solution.py:40
  7.8 2.7 %collective-permute-start.1 = (f32[192,128]{1,0:T(8,128)S(1)}, f32[192,128]{1,0:T(8,128)S(1)}, u32[]{:S(2)}, u32[]{:S(2)}) collective-permute-start(f32[192,128]{1,0:T(8,128)S(1)} %get-tuple-element.31), channel_id=1, source_target_pairs={{0,2},{2,0},{4,6},{6,4},{1,3},{3,1},{5,7},{7,5},{8,10},{10,8},{12,... | collective-permute-start | bytes 294920 | tf_op jit(solution)/shard_map/ppermute | solution.py:298
  10.5 1.5 %collective-permute-start.2 = (f32[192,128]{1,0:T(8,128)S(1)}, f32[192,128]{1,0:T(8,128)S(1)}, u32[]{:S(2)}, u32[]{:S(2)}) collective-permute-start(f32[192,128]{1,0:T(8,128)S(1)} %get-tuple-element.32), channel_id=1, source_target_pairs={{0,4},{2,6},{4,0},{6,2},{1,5},{3,7},{5,1},{7,3},{8,12},{10,14},{12... | collective-permute-start | bytes 294920 | tf_op jit(solution)/shard_map/ppermute | solution.py:298
  12.1 1.8 %collective-permute-done.1.refs_1_ = f32[192,128]{1,0:T(8,128)S(1)} collective-permute-done((f32[192,128]{1,0:T(8,128)S(1)}, f32[192,128]{1,0:T(8,128)S(1)}, u32[]{:S(2)}, u32[]{:S(2)}) %collective-permute-start.1) | collective-permute-done | bytes 98336 | tf_op jit(solution)/shard_map/ppermute | solution.py:298
  13.8 2.6 %collective-permute-done.2.refs_2_ = f32[192,128]{1,0:T(8,128)S(1)} collective-permute-done((f32[192,128]{1,0:T(8,128)S(1)}, f32[192,128]{1,0:T(8,128)S(1)}, u32[]{:S(2)}, u32[]{:S(2)}) %collective-permute-start.2) | collective-permute-done | bytes 98336 | tf_op jit(solution)/shard_map/ppermute | solution.py:298
  16.4 1.1 %collective-permute-done.3.refs_3_ = f32[192,128]{1,0:T(8,128)S(1)} collective-permute-done((f32[192,128]{1,0:T(8,128)S(1)}, f32[192,128]{1,0:T(8,128)S(1)}, u32[]{:S(2)}, u32[]{:S(2)}) %collective-permute-start.3) | collective-permute-done | bytes 98336 | tf_op jit(solution)/shard_map/ppermute | solution.py:298
  17.6 1.6 %collective-permute-start.4 = (f32[192,128]{1,0:T(8,128)S(1)}, f32[192,128]{1,0:T(8,128)S(1)}, u32[]{:S(2)}, u32[]{:S(2)}) collective-permute-start(f32[192,128]{1,0:T(8,128)S(1)} %shard_map.71.refs_0_), channel_id=1, source_target_pairs={{0,8},{8,0},{16,24},{24,16},{1,9},{9,1},{17,25},{25,17},{2,10},{10... | collective-permute-start | bytes 294920 | tf_op jit(solution)/shard_map/ppermute | solution.py:298
  19.2 2.6 %collective-permute-start.5 = (f32[192,128]{1,0:T(8,128)S(1)}, f32[192,128]{1,0:T(8,128)S(1)}, u32[]{:S(2)}, u32[]{:S(2)}) collective-permute-start(f32[192,128]{1,0:T(8,128)S(1)} %shard_map.71.refs_0_), channel_id=1, source_target_pairs={{0,16},{8,24},{16,0},{24,8},{1,17},{9,25},{17,1},{25,9},{2,18},{10... | collective-permute-start | bytes 294920 | tf_op jit(solution)/shard_map/ppermute | solution.py:298
  22.0 1.1 %collective-permute-done.4.refs_1_ = f32[192,128]{1,0:T(8,128)S(1)} collective-permute-done((f32[192,128]{1,0:T(8,128)S(1)}, f32[192,128]{1,0:T(8,128)S(1)}, u32[]{:S(2)}, u32[]{:S(2)}) %collective-permute-start.4) | collective-permute-done | bytes 98336 | tf_op jit(solution)/shard_map/ppermute | solution.py:298
  23.1 5.3 %collective-permute-done.5.refs_2_ = f32[192,128]{1,0:T(8,128)S(1)} collective-permute-done((f32[192,128]{1,0:T(8,128)S(1)}, f32[192,128]{1,0:T(8,128)S(1)}, u32[]{:S(2)}, u32[]{:S(2)}) %collective-permute-start.5) | collective-permute-done | bytes 98336 | tf_op jit(solution)/shard_map/ppermute | solution.py:298
  28.5 1.3 %collective-permute-start.9 = (f32[192,128]{1,0:T(8,128)S(1)}, f32[192,128]{1,0:T(8,128)S(1)}, u32[]{:S(2)}, u32[]{:S(2)}) collective-permute-start(f32[192,128]{1,0:T(8,128)S(1)} %shard_map.72.refs_0_), channel_id=1, source_target_pairs={{0,4},{2,6},{4,0},{6,2},{1,5},{3,7},{5,1},{7,3},{8,12},{10,14},{12... | collective-permute-start | bytes 294920 | tf_op jit(solution)/shard_map/ppermute | solution.py:298
  29.8 2.2 %collective-permute-start.11 = (f32[192,128]{1,0:T(8,128)S(1)}, f32[192,128]{1,0:T(8,128)S(1)}, u32[]{:S(2)}, u32[]{:S(2)}) collective-permute-start(f32[192,128]{1,0:T(8,128)S(1)} %shard_map.72.refs_0_), channel_id=1, source_target_pairs={{0,6},{2,4},{4,2},{6,0},{1,7},{3,5},{5,3},{7,1},{8,14},{10,12},{12... | collective-permute-start | bytes 294920 | tf_op jit(solution)/shard_map/ppermute | solution.py:298
  32.0 1.1 %collective-permute-done.9.refs_2_ = f32[192,128]{1,0:T(8,128)S(1)} collective-permute-done((f32[192,128]{1,0:T(8,128)S(1)}, f32[192,128]{1,0:T(8,128)S(1)}, u32[]{:S(2)}, u32[]{:S(2)}) %collective-permute-start.9) | collective-permute-done | bytes 98336 | tf_op jit(solution)/shard_map/ppermute | solution.py:298
  33.2 2.1 %collective-permute-done.11.refs_3_ = f32[192,128]{1,0:T(8,128)S(1)} collective-permute-done((f32[192,128]{1,0:T(8,128)S(1)}, f32[192,128]{1,0:T(8,128)S(1)}, u32[]{:S(2)}, u32[]{:S(2)}) %collective-permute-start.11) | collective-permute-done | bytes 98336 | tf_op jit(solution)/shard_map/ppermute | solution.py:298
  35.3 1.3 %collective-permute-done.7.refs_1_ = f32[192,128]{1,0:T(8,128)S(1)} collective-permute-done((f32[192,128]{1,0:T(8,128)S(1)}, f32[192,128]{1,0:T(8,128)S(1)}, u32[]{:S(2)}, u32[]{:S(2)}) %collective-permute-start.7) | collective-permute-done | bytes 98336 | tf_op jit(solution)/shard_map/ppermute | solution.py:298
  36.6 2.2 %shard_map.73 = (f32[3072,512]{1,0:T(8,128)S(1)}, bf16[6144,512]{1,0:T(8,128)(2,1)S(1)}) custom-call(bf16[512,3072]{1,0:T(8,128)(2,1)S(1)} %get-tuple-element.25.xv, bf16[512,512]{1,0:T(8,128)(2,1)S(1)} %copy-done, bf16[3072,512]{1,0:T(8,128)(2,1)S(1)} %get-tuple-element.26.ev), custom_call_target="tpu_custom_call" | custom-call | flops 1000000000 | tf_op jit(solution)/shard_map/pallas_call | solution.py:40
  39.7 1.4 %shard_map.75 = (bf16[192,1536]{1,0:T(8,128)(2,1)S(1)}, f32[192,512]{1,0:T(8,128)S(1)}) custom-call(s32[2]{0:T(128)S(1)} %pad_add_fusion.ids, f32[192,128]{1,0:T(8,128)S(1)} %collective-permute-done.13.refs_0_, f32[192,128]{1,0:T(8,128)S(1)} %collective-permute-done.7.refs_1_, f32[192,128]{1,0:T(8,128)S(1)} %collective-permute-done.9.refs_2_, ...), custom_call_target="tpu_custom_call" | custom-call | flops 100000000 | tf_op jit(solution)/shard_map/pallas_call | solution.py:40
  41.1 1.2 %shard_map.76 = (bf16[192,1152]{1,0:T(8,128)(2,1)S(1)}, f32[128,128]{1,0:T(8,128)S(1)}, f32[128,128]{1,0:T(8,128)S(1)}) custom-call(s32[2]{0:T(128)S(1)} %pad_add_fusion.ids, f32[192,128]{1,0:T(8,128)S(1)} %collective-permute-done.8.refs_0_, f32[192,128]{1,0:T(8,128)S(1)} %collective-permute-done.10.refs_1_, f32[192,128]{1,0:T(8,128)S(1)} %collective-permute-done.12.refs_2_, ...), custom_call_target="tpu_custom_call" | custom-call | flops 100000000 | tf_op jit(solution)/shard_map/pallas_call | solution.py:40
  43.8 1.1 %collective-permute-start.15 = (f32[128,128]{1,0:T(8,128)S(1)}, f32[128,128]{1,0:T(8,128)S(1)}, u32[]{:S(2)}, u32[]{:S(2)}) collective-permute-start(f32[128,128]{1,0:T(8,128)S(1)} %shard_map.77.refs_0_), channel_id=1, source_target_pairs={{0,2},{2,0},{4,6},{6,4},{1,3},{3,1},{5,7},{7,5},{8,10},{10,8},{12,... | collective-permute-start | bytes 196616 | tf_op jit(solution)/shard_map/ppermute | solution.py:298
  45.7 1.7 %collective-permute-start.17 = (f32[128,128]{1,0:T(8,128)S(1)}, f32[128,128]{1,0:T(8,128)S(1)}, u32[]{:S(2)}, u32[]{:S(2)}) collective-permute-start(f32[128,128]{1,0:T(8,128)S(1)} %shard_map.77.refs_0_), channel_id=1, source_target_pairs={{0,6},{2,4},{4,2},{6,0},{1,7},{3,5},{5,3},{7,1},{8,14},{10,12},{12... | collective-permute-start | bytes 196616 | tf_op jit(solution)/shard_map/ppermute | solution.py:298
  48.2 1.7 %collective-permute-done.16.refs_2_ = f32[128,128]{1,0:T(8,128)S(1)} collective-permute-done((f32[128,128]{1,0:T(8,128)S(1)}, f32[128,128]{1,0:T(8,128)S(1)}, u32[]{:S(2)}, u32[]{:S(2)}) %collective-permute-start.16) | collective-permute-done | bytes 65568 | tf_op jit(solution)/shard_map/ppermute | solution.py:298
  49.9 1.0 %collective-permute-done.17.refs_3_ = f32[128,128]{1,0:T(8,128)S(1)} collective-permute-done((f32[128,128]{1,0:T(8,128)S(1)}, f32[128,128]{1,0:T(8,128)S(1)}, u32[]{:S(2)}, u32[]{:S(2)}) %collective-permute-start.17) | collective-permute-done | bytes 65568 | tf_op jit(solution)/shard_map/ppermute | solution.py:298
  50.9 1.7 %collective-permute-start.18 = (f32[128,128]{1,0:T(8,128)S(1)}, f32[128,128]{1,0:T(8,128)S(1)}, u32[]{:S(2)}, u32[]{:S(2)}) collective-permute-start(f32[128,128]{1,0:T(8,128)S(1)} %shard_map.78.refs_0_), channel_id=1, source_target_pairs={{0,8},{8,0},{16,24},{24,16},{1,9},{9,1},{17,25},{25,17},{2,10},{10... | collective-permute-start | bytes 196616 | tf_op jit(solution)/shard_map/ppermute | solution.py:298
  52.5 1.4 %collective-permute-start.19 = (f32[128,128]{1,0:T(8,128)S(1)}, f32[128,128]{1,0:T(8,128)S(1)}, u32[]{:S(2)}, u32[]{:S(2)}) collective-permute-start(f32[128,128]{1,0:T(8,128)S(1)} %shard_map.78.refs_0_), channel_id=1, source_target_pairs={{0,16},{8,24},{16,0},{24,8},{1,17},{9,25},{17,1},{25,9},{2,18},{10... | collective-permute-start | bytes 196616 | tf_op jit(solution)/shard_map/ppermute | solution.py:298
  54.0 1.3 %collective-permute-start.20 = (f32[128,128]{1,0:T(8,128)S(1)}, f32[128,128]{1,0:T(8,128)S(1)}, u32[]{:S(2)}, u32[]{:S(2)}) collective-permute-start(f32[128,128]{1,0:T(8,128)S(1)} %shard_map.78.refs_0_), channel_id=1, source_target_pairs={{0,24},{8,16},{16,8},{24,0},{1,25},{9,17},{17,9},{25,1},{2,26},{10... | collective-permute-start | bytes 196616 | tf_op jit(solution)/shard_map/ppermute | solution.py:298
  55.3 2.0 %shard_map.81.refs_3_.lower_inv = f32[64,64]{1,0:T(8,128)S(1)} custom-call(f32[64,64]{1,0:T(8,128)S(1)} %shard_map.80.gram), custom_call_target="tpu_custom_call" | custom-call | flops 1000000000 | tf_op jit(solution)/shard_map/pallas_call | solution.py:40
  57.3 1.4 %collective-permute-done.19.refs_2_ = f32[128,128]{1,0:T(8,128)S(1)} collective-permute-done((f32[128,128]{1,0:T(8,128)S(1)}, f32[128,128]{1,0:T(8,128)S(1)}, u32[]{:S(2)}, u32[]{:S(2)}) %collective-permute-start.19) | collective-permute-done | bytes 65568 | tf_op jit(solution)/shard_map/ppermute | solution.py:298
  58.7 1.4 %collective-permute-done.20.refs_3_ = f32[128,128]{1,0:T(8,128)S(1)} collective-permute-done((f32[128,128]{1,0:T(8,128)S(1)}, f32[128,128]{1,0:T(8,128)S(1)}, u32[]{:S(2)}, u32[]{:S(2)}) %collective-permute-start.20) | collective-permute-done | bytes 65568 | tf_op jit(solution)/shard_map/ppermute | solution.py:298
  60.2 2.5 %shard_map.82 = (f32[64,3072]{1,0:T(8,128)}, bf16[3072,192]{1,0:T(8,128)(2,1)S(1)}) custom-call(s32[2]{0:T(128)S(1)} %pad_add_fusion.ids, bf16[192,384]{1,0:T(8,128)(2,1)S(1)} %get-tuple-element.39.refs_0_, bf16[192,1536]{1,0:T(8,128)(2,1)S(1)} %get-tuple-element.40.refs_1_, bf16[192,1152]{1,0:T(8,128)(2,1)S(1)} %get-tuple-element.41.refs_2_, ...), custom_call_target="tpu_custom_call" | custom-call | flops 1000000000 | tf_op jit(solution)/shard_map/pallas_call | solution.py:40
  62.7 2.8 %shard_map.83 = (bf16[1,3072,512]{2,1,0:T(8,128)(2,1)}, f32[64,512]{1,0:T(8,128)}) custom-call(s32[2]{0:T(128)S(1)} %pad_add_fusion.ids, f32[128,128]{1,0:T(8,128)S(1)} %shard_map.79.keep, f32[128,128]{1,0:T(8,128)S(1)} %collective-permute-done.21.other, f32[64,64]{1,0:T(8,128)S(1)} %shard_map.81.refs_3_.lower_inv, ...), custom_call_target="tpu_custom_call" | custom-call | flops 1000000000 | tf_op jit(solution)/shard_map/pallas_call | solution.py:40
  (34 shorter events, 5.2 us)
Async XLA Ops:
  0.7 1.6 %copy-start = (bf16[512,512]{1,0:T(8,128)(2,1)S(1)}, bf16[512,512]{1,0:T(8,128)(2,1)}, u32[]{:S(2)}) copy-start(bf16[512,512]{1,0:T(8,128)(2,1)} %yv.1) | copy-start | bytes 1572868
  0.7 1.6 %copy-start.1 = (f32[512,64]{0,1:T(8,128)S(1)}, f32[512,64]{0,1:T(8,128)}, u32[]{:S(2)}) copy-start(f32[512,64]{0,1:T(8,128)} %param.7) | copy-start | bytes 393220
  5.6 2.1 %collective-permute-start = (f32[768,128]{1,0:T(8,128)S(1)}, f32[768,128]{1,0:T(8,128)S(1)}, u32[]{:S(2)}, u32[]{:S(2)}) collective-permute-start(f32[768,128]{1,0:T(8,128)S(1)} %get-tuple-element.29), channel_id=1, source_target_pairs={{0,1},{1,0},{2,3},{3,2},{4,5},{5,4},{6,7},{7,6},{8,9},{9,8},{10,11... | collective-permute-start | bytes 1179656 | tf_op jit(solution)/shard_map/ppermute | solution.py:298
  7.8 6.0 %collective-permute-start.1 = (f32[192,128]{1,0:T(8,128)S(1)}, f32[192,128]{1,0:T(8,128)S(1)}, u32[]{:S(2)}, u32[]{:S(2)}) collective-permute-start(f32[192,128]{1,0:T(8,128)S(1)} %get-tuple-element.31), channel_id=1, source_target_pairs={{0,2},{2,0},{4,6},{6,4},{1,3},{3,1},{5,7},{7,5},{8,10},{10,8},{12,... | collective-permute-start | bytes 294920 | tf_op jit(solution)/shard_map/ppermute | solution.py:298
  10.5 5.9 %collective-permute-start.2 = (f32[192,128]{1,0:T(8,128)S(1)}, f32[192,128]{1,0:T(8,128)S(1)}, u32[]{:S(2)}, u32[]{:S(2)}) collective-permute-start(f32[192,128]{1,0:T(8,128)S(1)} %get-tuple-element.32), channel_id=1, source_target_pairs={{0,4},{2,6},{4,0},{6,2},{1,5},{3,7},{5,1},{7,3},{8,12},{10,14},{12... | collective-permute-start | bytes 294920 | tf_op jit(solution)/shard_map/ppermute | solution.py:298
  12.0 5.5 %collective-permute-start.3 = (f32[192,128]{1,0:T(8,128)S(1)}, f32[192,128]{1,0:T(8,128)S(1)}, u32[]{:S(2)}, u32[]{:S(2)}) collective-permute-start(f32[192,128]{1,0:T(8,128)S(1)} %get-tuple-element.33), channel_id=1, source_target_pairs={{0,6},{2,4},{4,2},{6,0},{1,7},{3,5},{5,3},{7,1},{8,14},{10,12},{12... | collective-permute-start | bytes 294920 | tf_op jit(solution)/shard_map/ppermute | solution.py:298
  17.6 5.5 %collective-permute-start.4 = (f32[192,128]{1,0:T(8,128)S(1)}, f32[192,128]{1,0:T(8,128)S(1)}, u32[]{:S(2)}, u32[]{:S(2)}) collective-permute-start(f32[192,128]{1,0:T(8,128)S(1)} %shard_map.71.refs_0_), channel_id=1, source_target_pairs={{0,8},{8,0},{16,24},{24,16},{1,9},{9,1},{17,25},{25,17},{2,10},{10... | collective-permute-start | bytes 294920 | tf_op jit(solution)/shard_map/ppermute | solution.py:298
  19.2 9.2 %collective-permute-start.5 = (f32[192,128]{1,0:T(8,128)S(1)}, f32[192,128]{1,0:T(8,128)S(1)}, u32[]{:S(2)}, u32[]{:S(2)}) collective-permute-start(f32[192,128]{1,0:T(8,128)S(1)} %shard_map.71.refs_0_), channel_id=1, source_target_pairs={{0,16},{8,24},{16,0},{24,8},{1,17},{9,25},{17,1},{25,9},{2,18},{10... | collective-permute-start | bytes 294920 | tf_op jit(solution)/shard_map/ppermute | solution.py:298
  21.8 6.7 %collective-permute-start.6 = (f32[192,128]{1,0:T(8,128)S(1)}, f32[192,128]{1,0:T(8,128)S(1)}, u32[]{:S(2)}, u32[]{:S(2)}) collective-permute-start(f32[192,128]{1,0:T(8,128)S(1)} %shard_map.71.refs_0_), channel_id=1, source_target_pairs={{0,24},{8,16},{16,8},{24,0},{1,25},{9,17},{17,9},{25,1},{2,26},{10... | collective-permute-start | bytes 294920 | tf_op jit(solution)/shard_map/ppermute | solution.py:298
  28.5 4.7 %collective-permute-start.9 = (f32[192,128]{1,0:T(8,128)S(1)}, f32[192,128]{1,0:T(8,128)S(1)}, u32[]{:S(2)}, u32[]{:S(2)}) collective-permute-start(f32[192,128]{1,0:T(8,128)S(1)} %shard_map.72.refs_0_), channel_id=1, source_target_pairs={{0,4},{2,6},{4,0},{6,2},{1,5},{3,7},{5,1},{7,3},{8,12},{10,14},{12... | collective-permute-start | bytes 294920 | tf_op jit(solution)/shard_map/ppermute | solution.py:298
  29.8 5.5 %collective-permute-start.11 = (f32[192,128]{1,0:T(8,128)S(1)}, f32[192,128]{1,0:T(8,128)S(1)}, u32[]{:S(2)}, u32[]{:S(2)}) collective-permute-start(f32[192,128]{1,0:T(8,128)S(1)} %shard_map.72.refs_0_), channel_id=1, source_target_pairs={{0,6},{2,4},{4,2},{6,0},{1,7},{3,5},{5,3},{7,1},{8,14},{10,12},{12... | collective-permute-start | bytes 294920 | tf_op jit(solution)/shard_map/ppermute | solution.py:298
  32.0 4.6 %collective-permute-start.7 = (f32[192,128]{1,0:T(8,128)S(1)}, f32[192,128]{1,0:T(8,128)S(1)}, u32[]{:S(2)}, u32[]{:S(2)}) collective-permute-start(f32[192,128]{1,0:T(8,128)S(1)} %shard_map.72.refs_0_), channel_id=1, source_target_pairs={{0,2},{2,0},{4,6},{6,4},{1,3},{3,1},{5,7},{7,5},{8,10},{10,8},{12,... | collective-permute-start | bytes 294920 | tf_op jit(solution)/shard_map/ppermute | solution.py:298
  32.0 7.6 %collective-permute-start.13 = (f32[192,128]{1,0:T(8,128)S(1)}, f32[192,128]{1,0:T(8,128)S(1)}, u32[]{:S(2)}, u32[]{:S(2)}) collective-permute-start(f32[192,128]{1,0:T(8,128)S(1)} %shard_map.72.refs_0_), channel_id=1, source_target_pairs={{0,1},{1,0},{2,3},{3,2},{4,5},{5,4},{6,7},{7,6},{8,9},{9,8},{10,11... | collective-permute-start | bytes 294920 | tf_op jit(solution)/shard_map/ppermute | solution.py:298
  33.2 7.9 %collective-permute-start.10 = (f32[192,128]{1,0:T(8,128)S(1)}, f32[192,128]{1,0:T(8,128)S(1)}, u32[]{:S(2)}, u32[]{:S(2)}) collective-permute-start(f32[192,128]{1,0:T(8,128)S(1)} %collective-permute-done.9.refs_2_), channel_id=1, source_target_pairs={{0,1},{1,0},{2,3},{3,2},{4,5},{5,4},{6,7},{7,6},{8,9},{9,8},{10,11... | collective-permute-start | bytes 294920 | tf_op jit(solution)/shard_map/ppermute | solution.py:298
  35.3 5.8 %collective-permute-start.12 = (f32[192,128]{1,0:T(8,128)S(1)}, f32[192,128]{1,0:T(8,128)S(1)}, u32[]{:S(2)}, u32[]{:S(2)}) collective-permute-start(f32[192,128]{1,0:T(8,128)S(1)} %collective-permute-done.11.refs_3_), channel_id=1, source_target_pairs={{0,1},{1,0},{2,3},{3,2},{4,5},{5,4},{6,7},{7,6},{8,9},{9,8},{10,11... | collective-permute-start | bytes 294920 | tf_op jit(solution)/shard_map/ppermute | solution.py:298
  36.6 4.5 %collective-permute-start.8 = (f32[192,128]{1,0:T(8,128)S(1)}, f32[192,128]{1,0:T(8,128)S(1)}, u32[]{:S(2)}, u32[]{:S(2)}) collective-permute-start(f32[192,128]{1,0:T(8,128)S(1)} %collective-permute-done.7.refs_1_), channel_id=1, source_target_pairs={{0,1},{1,0},{2,3},{3,2},{4,5},{5,4},{6,7},{7,6},{8,9},{9,8},{10,11... | collective-permute-start | bytes 294920 | tf_op jit(solution)/shard_map/ppermute | solution.py:298
  42.3 1.5 %collective-permute-start.14 = (f32[128,128]{1,0:T(8,128)S(1)}, f32[128,128]{1,0:T(8,128)S(1)}, u32[]{:S(2)}, u32[]{:S(2)}) collective-permute-start(f32[128,128]{1,0:T(8,128)S(1)} %get-tuple-element.38), channel_id=1, source_target_pairs={{0,1},{1,0},{2,3},{3,2},{4,5},{5,4},{6,7},{7,6},{8,9},{9,8},{10,11... | collective-permute-start | bytes 196616 | tf_op jit(solution)/shard_map/ppermute | solution.py:298
  43.8 4.4 %collective-permute-start.15 = (f32[128,128]{1,0:T(8,128)S(1)}, f32[128,128]{1,0:T(8,128)S(1)}, u32[]{:S(2)}, u32[]{:S(2)}) collective-permute-start(f32[128,128]{1,0:T(8,128)S(1)} %shard_map.77.refs_0_), channel_id=1, source_target_pairs={{0,2},{2,0},{4,6},{6,4},{1,3},{3,1},{5,7},{7,5},{8,10},{10,8},{12,... | collective-permute-start | bytes 196616 | tf_op jit(solution)/shard_map/ppermute | solution.py:298
  44.9 5.0 %collective-permute-start.16 = (f32[128,128]{1,0:T(8,128)S(1)}, f32[128,128]{1,0:T(8,128)S(1)}, u32[]{:S(2)}, u32[]{:S(2)}) collective-permute-start(f32[128,128]{1,0:T(8,128)S(1)} %shard_map.77.refs_0_), channel_id=1, source_target_pairs={{0,4},{2,6},{4,0},{6,2},{1,5},{3,7},{5,1},{7,3},{8,12},{10,14},{12... | collective-permute-start | bytes 196616 | tf_op jit(solution)/shard_map/ppermute | solution.py:298
  45.7 5.2 %collective-permute-start.17 = (f32[128,128]{1,0:T(8,128)S(1)}, f32[128,128]{1,0:T(8,128)S(1)}, u32[]{:S(2)}, u32[]{:S(2)}) collective-permute-start(f32[128,128]{1,0:T(8,128)S(1)} %shard_map.77.refs_0_), channel_id=1, source_target_pairs={{0,6},{2,4},{4,2},{6,0},{1,7},{3,5},{5,3},{7,1},{8,14},{10,12},{12... | collective-permute-start | bytes 196616 | tf_op jit(solution)/shard_map/ppermute | solution.py:298
  50.9 6.4 %collective-permute-start.18 = (f32[128,128]{1,0:T(8,128)S(1)}, f32[128,128]{1,0:T(8,128)S(1)}, u32[]{:S(2)}, u32[]{:S(2)}) collective-permute-start(f32[128,128]{1,0:T(8,128)S(1)} %shard_map.78.refs_0_), channel_id=1, source_target_pairs={{0,8},{8,0},{16,24},{24,16},{1,9},{9,1},{17,25},{25,17},{2,10},{10... | collective-permute-start | bytes 196616 | tf_op jit(solution)/shard_map/ppermute | solution.py:298
  52.5 6.1 %collective-permute-start.19 = (f32[128,128]{1,0:T(8,128)S(1)}, f32[128,128]{1,0:T(8,128)S(1)}, u32[]{:S(2)}, u32[]{:S(2)}) collective-permute-start(f32[128,128]{1,0:T(8,128)S(1)} %shard_map.78.refs_0_), channel_id=1, source_target_pairs={{0,16},{8,24},{16,0},{24,8},{1,17},{9,25},{17,1},{25,9},{2,18},{10... | collective-permute-start | bytes 196616 | tf_op jit(solution)/shard_map/ppermute | solution.py:298
  54.0 6.1 %collective-permute-start.20 = (f32[128,128]{1,0:T(8,128)S(1)}, f32[128,128]{1,0:T(8,128)S(1)}, u32[]{:S(2)}, u32[]{:S(2)}) collective-permute-start(f32[128,128]{1,0:T(8,128)S(1)} %shard_map.78.refs_0_), channel_id=1, source_target_pairs={{0,24},{8,16},{16,8},{24,0},{1,25},{9,17},{17,9},{25,1},{2,26},{10... | collective-permute-start | bytes 196616 | tf_op jit(solution)/shard_map/ppermute | solution.py:298
  60.1 2.6 %collective-permute-start.21 = (f32[128,128]{1,0:T(8,128)S(1)}, f32[128,128]{1,0:T(8,128)S(1)}, u32[]{:S(2)}, u32[]{:S(2)}) collective-permute-start(f32[128,128]{1,0:T(8,128)S(1)} %shard_map.79.keep), channel_id=1, source_target_pairs={{0,1},{1,0},{2,3},{3,2},{4,5},{5,4},{6,7},{7,6},{8,9},{9,8},{10,11... | collective-permute-start | bytes 196616 | tf_op jit(solution)/shard_map/ppermute | solution.py:298
where the time goes:
time: 65.6 us; the launch traced here: 65.5 us
  waiting for transfers between devices  23.1 us (35%)
  starting transfers between devices  21.5 us (33%)
  Pallas kernels  20.1 us (31%)
  between operations  0.83 us (1%)
    ppermute x22, waiting for transfers between devices, swap(): return lax.ppermute(x, axis, [(i, i ^ by) for i in range(size)])  23.1 us
    ppermute x22, starting transfers between devices, swap(): return lax.ppermute(x, axis, [(i, i ^ by) for i in range(size)])  21.5 us
    pallas_call x17, Pallas kernels, call(): pl.pallas_call(kernel, out_shape=outs, in_specs=ins_specs, out_specs=out_...  20.1 us
  transfers between devices with their start and end apart: 22, of which 14 were waited for; matrix products, arithmetic and copies ran while one was open for 0% of the time, Pallas kernels for 17%

commit v1 on v0

--- a/solution.py
+++ b/solution.py
@@ -154,32 +154,47 @@
     return (where[0] ^ ids[0]) * chips + (where[1] ^ ids[1])
 
 
-def chunk_kernel(chips, places, first, last, ids, *refs):
-    parts, rest = refs[: len(places)], refs[len(places) :]
-    merged2, rest = rest[0], rest[1:]
-    before, rest = (None, rest) if first else (rest[0], rest[1:])
-    p3 = rest[0]
+def split_chunks(parts, p3):
     rank = p3.shape[0] // 3
-    span = parts[0].shape[0] // rank * LANES
-    t = None if first else before[...]
-    for i, (part, where) in enumerate(zip(parts, places)):
-        for c in range(span // LANES):
-            at = i * span + c * LANES
-            p3[:, at : at + LANES] = split3(part[c * rank : (c + 1) * rank, :])
+    for i in range(len(parts) * parts[0].shape[0] // rank):
+        part, c = parts[i * rank // parts[0].shape[0]], i % (parts[0].shape[0] // rank)
+        p3[:, i * LANES : (i + 1) * LANES] = split3(part[c * rank : (c + 1) * rank, :])
+
+
+def add_chunks(chips, places, ids, p3, merged2, columns, t):
+    span = p3.shape[1] // len(places)
+    for i, where in enumerate(places):
         rows = pl.ds(pl.multiple_of(chunk_of(chips, ids, where) * (2 * span), 16), 2 * span)
         mine = p3[:, i * span : (i + 1) * span]
-        new = dot(jnp.concatenate([mine, mine], axis=1), merged2[rows, :], NN)
+        new = dot(jnp.concatenate([mine, mine], axis=1), merged2[rows, columns], NN)
         t = new if t is None else t + new
-    if not last:
-        rest[1][...] = t
-        return
-    keep, send, total = rest[1:]
-    right = fold3(t)
-    for c in range(right.shape[1] // LANES):
-        total[c * rank : (c + 1) * rank, :] = right[:, c * LANES : (c + 1) * LANES]
-    size = keep.shape[0]
-    keep[...] = total[pl.ds(pl.multiple_of(ids[0] * size, 8), size), :]
-    send[...] = total[pl.ds(pl.multiple_of((1 - ids[0]) * size, 8), size), :]
+    return t
+
+
+def chunk_kernel(chips, places, first, ids, *refs):
+    parts, rest = refs[: len(places)], refs[len(places) :]
+    merged2, (p3, t) = rest[0], rest[-2:]
+    split_chunks(parts, p3)
+    t[...] = add_chunks(chips, places, ids, p3, merged2, slice(None), None if first else rest[1][...])
+
+
+def half_of(chips, places, core, ids, p3, merged2, before, out):
+    rank = p3.shape[0] // 3
+    wide = out.shape[0] // rank * LANES
+    columns = pl.ds(pl.multiple_of(core * wide, LANES), wide)
+    right = fold3(add_chunks(chips, places, ids, p3, merged2, columns, before[:, columns]))
+    for c in range(wide // LANES):
+        out[c * rank : (c + 1) * rank, :] = right[:, c * LANES : (c + 1) * LANES]
+
+
+def send_kernel(chips, places, ids, *refs):
+    merged2, before, p3, send = refs[len(places) :]
+    split_chunks(refs[: len(places)], p3)
+    half_of(chips, places, 1 - ids[0], ids, p3, merged2, before, send)
+
+
+def keep_kernel(chips, places, ids, p3, merged2, before, keep):
+    half_of(chips, places, ids[0], ids, p3, merged2, before, keep)
 
 
 def gram_kernel(*refs):
@@ -369,22 +384,36 @@
     places = [(core, chip) for core in range(cores) for chip in range(chips)]
     batches = [[0], [chips, *range(1, chips)], list(range(chips + 1, 2 * chips))]
     share = vmem((width * rank // LANES // cores, LANES))
-    sums, p3s, order = [], [], []
+    t, p3s, order = [], [], []
     for at, batch in enumerate(batches):
+        where = [places[k] for k in batch]
+        arrived = [parts[k] for k in batch]
         end = at == len(batches) - 1
-        p3, *sums = call(
-            functools.partial(chunk_kernel, chips, [places[k] for k in batch], at == 0, end),
-            [vmem((3 * rank, span * len(batch)), BF16)] + ([share, share] if end else [vmem((3 * rank, width))]),
-            [SM] + [VM] * (len(batch) + 1 + len(sums)),
-            [VM] * (3 if end else 2),
-            [pltpu.VMEM((width * rank // LANES, LANES), F32)] if end else [],
-            (ids, *[parts[k] for k in batch], merged2, *sums),
+        p3, more = call(
+            functools.partial(send_kernel, chips, where) if end else functools.partial(chunk_kernel, chips, where, at == 0),
+            [vmem((3 * rank, span * len(batch)), BF16), share if end else vmem((3 * rank, width))],
+            [SM] + [VM] * (len(batch) + 1 + len(t)),
+            [VM] * 2,
+            [],
+            (ids, *arrived, merged2, *t),
             10**8,
             8,
         )
         p3s.append(p3)
-        order += [places[k] for k in batch]
-    keep, send = sums
+        order += where
+        if not end:
+            t = [more]
+    send = more
+    keep = call(
+        functools.partial(keep_kernel, chips, where),
+        share,
+        [SM] + [VM] * 3,
+        VM,
+        [],
+        (ids, p3s[-1], merged2, *t),
+        10**8,
+        8,
+    )
     got = swap(send, "core", cores, 1)
     part = add_up([keep, got], 1)[0]
     part = add_up(exchange([part] * chips, "chip", chips), 1)[0]

time: 65.6 us -> 65.4 us (level)
  waiting for transfers between devices: 23.1 us -> 22.1 us
  Pallas kernels: 20.1 us -> 20.8 us
    ppermute x22, waiting for transfers between devices: 23.1 us -> 22.1 us  [swap(): return lax.ppermute(x, axis, [(i, i ^ by) for i in range(size)])]
    pallas_call x17 -> x18, Pallas kernels: 20.1 us -> 20.8 us  [call(): pl.pallas_call(kernel, out_shape=outs, in_specs=ins_specs, out_specs=out_...]
  transfers between devices with their start and end apart: 22 -> 22, of which waited for: 14 -> 13; matrix products, arithmetic and copies ran while one was open for 0% -> 0% of each run, Pallas kernels for 17% -> 18%
where the time goes in v1:
time: 65.4 us; the launch traced here: 65.3 us
  waiting for transfers between devices  22.1 us (34%)
  starting transfers between devices  21.5 us (33%)
  Pallas kernels  20.8 us (32%)
  between operations  0.85 us (1%)
    ppermute x22, waiting for transfers between devices, swap(): return lax.ppermute(x, axis, [(i, i ^ by) for i in range(size)])  22.1 us
    ppermute x22, starting transfers between devices, swap(): return lax.ppermute(x, axis, [(i, i ^ by) for i in range(size)])  21.5 us
    pallas_call x18, Pallas kernels, call(): pl.pallas_call(kernel, out_shape=outs, in_specs=ins_specs, out_specs=out_...  20.8 us
  transfers between devices with their start and end apart: 22, of which 13 were waited for; matrix products, arithmetic and copies ran while one was open for 0% of the time, Pallas kernels for 18%

profile of v1, /device:TPU:0, one launch (start us, length us, event | category | flops | bytes accessed | tf_op | source)
XLA Modules:
  0.0 65.3 jit_solution(837592008742054589)
XLA Ops:
  0.7 1.6 %shard_map.67.e_in = bf16[3072,512]{1,0:T(8,128)(2,1)S(1)} custom-call(s32[2]{0:T(128)S(1)} %pad_add_fusion.ids, bf16[1,3072,512]{2,1,0:T(8,128)(2,1)} %e_hbm.3), custom_call_target="tpu_custom_call" | custom-call | flops 1000000000 | tf_op jit(solution)/shard_map/pallas_call | solution.py:40
  2.3 3.3 %shard_map.68 = (f32[768,128]{1,0:T(8,128)S(1)}, bf16[512,3072]{1,0:T(8,128)(2,1)S(1)}, bf16[3072,512]{1,0:T(8,128)(2,1)S(1)}, bf16[192,512]{1,0:T(8,128)(2,1)S(1)}, bf16[192,512]{1,0:T(8,128)(2,1)S(1)}) custom-call(s32[2]{0:T(128)S(1)} %pad_add_fusion.ids, bf16[512,3072]{1,0:T(8,128)(2,1)} %x_hbm.1, ...), custom_call_target="tpu_custom_call", output_to_operand_aliasing={{2}: (5, {})} | custom-call | flops 1000000000 | tf_op jit(solution)/shard_map/pallas_call | solution.py:40
  6.2 1.5 %shard_map.69.refs_0_ = f32[768,128]{1,0:T(8,128)S(1)} custom-call(s32[2]{0:T(128)S(1)} %pad_add_fusion.ids, bf16[512,3072]{1,0:T(8,128)(2,1)S(1)} %get-tuple-element.24.xv, bf16[3072,512]{1,0:T(8,128)(2,1)S(1)} %get-tuple-element.25.ev, bf16[192,512]{1,0:T(8,128)(2,1)S(1)} %get-tuple-element.26.v3, bf16[192,512]{1,0:T(8,128)(2,1)S(1)} %get-tuple-element.27.q3), custom_call_target="tpu_custom_call" | custom-call | flops 1000000000 | tf_op jit(solution)/shard_map/pallas_call | solution.py:40
  7.8 2.7 %collective-permute-start.1 = (f32[192,128]{1,0:T(8,128)S(1)}, f32[192,128]{1,0:T(8,128)S(1)}, u32[]{:S(2)}, u32[]{:S(2)}) collective-permute-start(f32[192,128]{1,0:T(8,128)S(1)} %get-tuple-element.30), channel_id=1, source_target_pairs={{0,2},{2,0},{4,6},{6,4},{1,3},{3,1},{5,7},{7,5},{8,10},{10,8},{12,... | collective-permute-start | bytes 294920 | tf_op jit(solution)/shard_map/ppermute | solution.py:313
  10.5 1.5 %collective-permute-start.2 = (f32[192,128]{1,0:T(8,128)S(1)}, f32[192,128]{1,0:T(8,128)S(1)}, u32[]{:S(2)}, u32[]{:S(2)}) collective-permute-start(f32[192,128]{1,0:T(8,128)S(1)} %get-tuple-element.31), channel_id=1, source_target_pairs={{0,4},{2,6},{4,0},{6,2},{1,5},{3,7},{5,1},{7,3},{8,12},{10,14},{12... | collective-permute-start | bytes 294920 | tf_op jit(solution)/shard_map/ppermute | solution.py:313
  12.1 1.8 %collective-permute-done.1.refs_1_ = f32[192,128]{1,0:T(8,128)S(1)} collective-permute-done((f32[192,128]{1,0:T(8,128)S(1)}, f32[192,128]{1,0:T(8,128)S(1)}, u32[]{:S(2)}, u32[]{:S(2)}) %collective-permute-start.1) | collective-permute-done | bytes 98336 | tf_op jit(solution)/shard_map/ppermute | solution.py:313
  13.8 2.6 %collective-permute-done.2.refs_2_ = f32[192,128]{1,0:T(8,128)S(1)} collective-permute-done((f32[192,128]{1,0:T(8,128)S(1)}, f32[192,128]{1,0:T(8,128)S(1)}, u32[]{:S(2)}, u32[]{:S(2)}) %collective-permute-start.2) | collective-permute-done | bytes 98336 | tf_op jit(solution)/shard_map/ppermute | solution.py:313
  16.4 1.1 %collective-permute-done.3.refs_3_ = f32[192,128]{1,0:T(8,128)S(1)} collective-permute-done((f32[192,128]{1,0:T(8,128)S(1)}, f32[192,128]{1,0:T(8,128)S(1)}, u32[]{:S(2)}, u32[]{:S(2)}) %collective-permute-start.3) | collective-permute-done | bytes 98336 | tf_op jit(solution)/shard_map/ppermute | solution.py:313
  17.6 1.6 %collective-permute-start.4 = (f32[192,128]{1,0:T(8,128)S(1)}, f32[192,128]{1,0:T(8,128)S(1)}, u32[]{:S(2)}, u32[]{:S(2)}) collective-permute-start(f32[192,128]{1,0:T(8,128)S(1)} %shard_map.71.refs_0_), channel_id=1, source_target_pairs={{0,8},{8,0},{16,24},{24,16},{1,9},{9,1},{17,25},{25,17},{2,10},{10... | collective-permute-start | bytes 294920 | tf_op jit(solution)/shard_map/ppermute | solution.py:313
  19.2 2.6 %collective-permute-start.5 = (f32[192,128]{1,0:T(8,128)S(1)}, f32[192,128]{1,0:T(8,128)S(1)}, u32[]{:S(2)}, u32[]{:S(2)}) collective-permute-start(f32[192,128]{1,0:T(8,128)S(1)} %shard_map.71.refs_0_), channel_id=1, source_target_pairs={{0,16},{8,24},{16,0},{24,8},{1,17},{9,25},{17,1},{25,9},{2,18},{10... | collective-permute-start | bytes 294920 | tf_op jit(solution)/shard_map/ppermute | solution.py:313
  22.0 1.1 %collective-permute-done.4.refs_1_ = f32[192,128]{1,0:T(8,128)S(1)} collective-permute-done((f32[192,128]{1,0:T(8,128)S(1)}, f32[192,128]{1,0:T(8,128)S(1)}, u32[]{:S(2)}, u32[]{:S(2)}) %collective-permute-start.4) | collective-permute-done | bytes 98336 | tf_op jit(solution)/shard_map/ppermute | solution.py:313
  23.1 5.3 %collective-permute-done.5.refs_2_ = f32[192,128]{1,0:T(8,128)S(1)} collective-permute-done((f32[192,128]{1,0:T(8,128)S(1)}, f32[192,128]{1,0:T(8,128)S(1)}, u32[]{:S(2)}, u32[]{:S(2)}) %collective-permute-start.5) | collective-permute-done | bytes 98336 | tf_op jit(solution)/shard_map/ppermute | solution.py:313
  28.5 1.3 %collective-permute-start.9 = (f32[192,128]{1,0:T(8,128)S(1)}, f32[192,128]{1,0:T(8,128)S(1)}, u32[]{:S(2)}, u32[]{:S(2)}) collective-permute-start(f32[192,128]{1,0:T(8,128)S(1)} %shard_map.72.refs_0_), channel_id=1, source_target_pairs={{0,4},{2,6},{4,0},{6,2},{1,5},{3,7},{5,1},{7,3},{8,12},{10,14},{12... | collective-permute-start | bytes 294920 | tf_op jit(solution)/shard_map/ppermute | solution.py:313
  29.8 2.2 %collective-permute-start.11 = (f32[192,128]{1,0:T(8,128)S(1)}, f32[192,128]{1,0:T(8,128)S(1)}, u32[]{:S(2)}, u32[]{:S(2)}) collective-permute-start(f32[192,128]{1,0:T(8,128)S(1)} %shard_map.72.refs_0_), channel_id=1, source_target_pairs={{0,6},{2,4},{4,2},{6,0},{1,7},{3,5},{5,3},{7,1},{8,14},{10,12},{12... | collective-permute-start | bytes 294920 | tf_op jit(solution)/shard_map/ppermute | solution.py:313
  32.0 1.1 %collective-permute-done.9.refs_2_ = f32[192,128]{1,0:T(8,128)S(1)} collective-permute-done((f32[192,128]{1,0:T(8,128)S(1)}, f32[192,128]{1,0:T(8,128)S(1)}, u32[]{:S(2)}, u32[]{:S(2)}) %collective-permute-start.9) | collective-permute-done | bytes 98336 | tf_op jit(solution)/shard_map/ppermute | solution.py:313
  33.2 2.1 %collective-permute-done.11.refs_3_ = f32[192,128]{1,0:T(8,128)S(1)} collective-permute-done((f32[192,128]{1,0:T(8,128)S(1)}, f32[192,128]{1,0:T(8,128)S(1)}, u32[]{:S(2)}, u32[]{:S(2)}) %collective-permute-start.11) | collective-permute-done | bytes 98336 | tf_op jit(solution)/shard_map/ppermute | solution.py:313
  35.3 1.3 %collective-permute-done.7.refs_1_ = f32[192,128]{1,0:T(8,128)S(1)} collective-permute-done((f32[192,128]{1,0:T(8,128)S(1)}, f32[192,128]{1,0:T(8,128)S(1)}, u32[]{:S(2)}, u32[]{:S(2)}) %collective-permute-start.7) | collective-permute-done | bytes 98336 | tf_op jit(solution)/shard_map/ppermute | solution.py:313
  36.6 2.2 %shard_map.73 = (f32[3072,512]{1,0:T(8,128)S(1)}, bf16[6144,512]{1,0:T(8,128)(2,1)S(1)}) custom-call(bf16[512,3072]{1,0:T(8,128)(2,1)S(1)} %get-tuple-element.24.xv, bf16[512,512]{1,0:T(8,128)(2,1)S(1)} %copy-done, bf16[3072,512]{1,0:T(8,128)(2,1)S(1)} %get-tuple-element.25.ev), custom_call_target="tpu_custom_call" | custom-call | flops 1000000000 | tf_op jit(solution)/shard_map/pallas_call | solution.py:40
  39.7 1.3 %shard_map.75 = (bf16[192,1536]{1,0:T(8,128)(2,1)S(1)}, f32[192,512]{1,0:T(8,128)S(1)}) custom-call(s32[2]{0:T(128)S(1)} %pad_add_fusion.ids, f32[192,128]{1,0:T(8,128)S(1)} %collective-permute-done.13.refs_0_, f32[192,128]{1,0:T(8,128)S(1)} %collective-permute-done.7.refs_1_, f32[192,128]{1,0:T(8,128)S(1)} %collective-permute-done.9.refs_2_, ...), custom_call_target="tpu_custom_call" | custom-call | flops 100000000 | tf_op jit(solution)/shard_map/pallas_call | solution.py:40
  41.1 1.0 %shard_map.76 = (bf16[192,1152]{1,0:T(8,128)(2,1)S(1)}, f32[128,128]{1,0:T(8,128)S(1)}) custom-call(s32[2]{0:T(128)S(1)} %pad_add_fusion.ids, f32[192,128]{1,0:T(8,128)S(1)} %collective-permute-done.8.refs_0_, f32[192,128]{1,0:T(8,128)S(1)} %collective-permute-done.10.refs_1_, f32[192,128]{1,0:T(8,128)S(1)} %collective-permute-done.12.refs_2_, ...), custom_call_target="tpu_custom_call" | custom-call | flops 100000000 | tf_op jit(solution)/shard_map/pallas_call | solution.py:40
  42.6 1.0 %shard_map.77.refs_0_ = f32[128,128]{1,0:T(8,128)S(1)} custom-call(s32[2]{0:T(128)S(1)} %pad_add_fusion.ids, bf16[192,1152]{1,0:T(8,128)(2,1)S(1)} %get-tuple-element.36.p3.refs_2_, bf16[6144,512]{1,0:T(8,128)(2,1)S(1)} %get-tuple-element.33.refs_1_.refs_4_.refs_3_.merged2, f32[192,512]{1,0:T(8,128)S(1)} %get-tuple-element.35.refs_4_.before), custom_call_target="tpu_custom_call" | custom-call | flops 100000000 | tf_op jit(solution)/shard_map/pallas_call | solution.py:40
  43.6 1.1 %collective-permute-start.15 = (f32[128,128]{1,0:T(8,128)S(1)}, f32[128,128]{1,0:T(8,128)S(1)}, u32[]{:S(2)}, u32[]{:S(2)}) collective-permute-start(f32[128,128]{1,0:T(8,128)S(1)} %shard_map.78.refs_0_), channel_id=1, source_target_pairs={{0,2},{2,0},{4,6},{6,4},{1,3},{3,1},{5,7},{7,5},{8,10},{10,8},{12,... | collective-permute-start | bytes 196616 | tf_op jit(solution)/shard_map/ppermute | solution.py:313
  45.4 1.8 %collective-permute-start.17 = (f32[128,128]{1,0:T(8,128)S(1)}, f32[128,128]{1,0:T(8,128)S(1)}, u32[]{:S(2)}, u32[]{:S(2)}) collective-permute-start(f32[128,128]{1,0:T(8,128)S(1)} %shard_map.78.refs_0_), channel_id=1, source_target_pairs={{0,6},{2,4},{4,2},{6,0},{1,7},{3,5},{5,3},{7,1},{8,14},{10,12},{12... | collective-permute-start | bytes 196616 | tf_op jit(solution)/shard_map/ppermute | solution.py:313
  48.0 1.7 %collective-permute-done.16.refs_2_ = f32[128,128]{1,0:T(8,128)S(1)} collective-permute-done((f32[128,128]{1,0:T(8,128)S(1)}, f32[128,128]{1,0:T(8,128)S(1)}, u32[]{:S(2)}, u32[]{:S(2)}) %collective-permute-start.16) | collective-permute-done | bytes 65568 | tf_op jit(solution)/shard_map/ppermute | solution.py:313
  50.6 1.7 %collective-permute-start.18 = (f32[128,128]{1,0:T(8,128)S(1)}, f32[128,128]{1,0:T(8,128)S(1)}, u32[]{:S(2)}, u32[]{:S(2)}) collective-permute-start(f32[128,128]{1,0:T(8,128)S(1)} %shard_map.79.refs_0_), channel_id=1, source_target_pairs={{0,8},{8,0},{16,24},{24,16},{1,9},{9,1},{17,25},{25,17},{2,10},{10... | collective-permute-start | bytes 196616 | tf_op jit(solution)/shard_map/ppermute | solution.py:313
  52.3 1.4 %collective-permute-start.19 = (f32[128,128]{1,0:T(8,128)S(1)}, f32[128,128]{1,0:T(8,128)S(1)}, u32[]{:S(2)}, u32[]{:S(2)}) collective-permute-start(f32[128,128]{1,0:T(8,128)S(1)} %shard_map.79.refs_0_), channel_id=1, source_target_pairs={{0,16},{8,24},{16,0},{24,8},{1,17},{9,25},{17,1},{25,9},{2,18},{10... | collective-permute-start | bytes 196616 | tf_op jit(solution)/shard_map/ppermute | solution.py:313
  53.7 1.3 %collective-permute-start.20 = (f32[128,128]{1,0:T(8,128)S(1)}, f32[128,128]{1,0:T(8,128)S(1)}, u32[]{:S(2)}, u32[]{:S(2)}) collective-permute-start(f32[128,128]{1,0:T(8,128)S(1)} %shard_map.79.refs_0_), channel_id=1, source_target_pairs={{0,24},{8,16},{16,8},{24,0},{1,25},{9,17},{17,9},{25,1},{2,26},{10... | collective-permute-start | bytes 196616 | tf_op jit(solution)/shard_map/ppermute | solution.py:313
  55.1 2.0 %shard_map.82.refs_3_.lower_inv = f32[64,64]{1,0:T(8,128)S(1)} custom-call(f32[64,64]{1,0:T(8,128)S(1)} %shard_map.81.gram), custom_call_target="tpu_custom_call" | custom-call | flops 1000000000 | tf_op jit(solution)/shard_map/pallas_call | solution.py:40
  57.0 1.5 %collective-permute-done.19.refs_2_ = f32[128,128]{1,0:T(8,128)S(1)} collective-permute-done((f32[128,128]{1,0:T(8,128)S(1)}, f32[128,128]{1,0:T(8,128)S(1)}, u32[]{:S(2)}, u32[]{:S(2)}) %collective-permute-start.19) | collective-permute-done | bytes 65568 | tf_op jit(solution)/shard_map/ppermute | solution.py:313
  58.5 1.4 %collective-permute-done.20.refs_3_ = f32[128,128]{1,0:T(8,128)S(1)} collective-permute-done((f32[128,128]{1,0:T(8,128)S(1)}, f32[128,128]{1,0:T(8,128)S(1)}, u32[]{:S(2)}, u32[]{:S(2)}) %collective-permute-start.20) | collective-permute-done | bytes 65568 | tf_op jit(solution)/shard_map/ppermute | solution.py:313
  60.0 2.5 %shard_map.83 = (f32[64,3072]{1,0:T(8,128)}, bf16[3072,192]{1,0:T(8,128)(2,1)S(1)}) custom-call(s32[2]{0:T(128)S(1)} %pad_add_fusion.ids, bf16[192,384]{1,0:T(8,128)(2,1)S(1)} %get-tuple-element.38.refs_0_, bf16[192,1536]{1,0:T(8,128)(2,1)S(1)} %get-tuple-element.39.refs_1_, bf16[192,1152]{1,0:T(8,128)(2,1)S(1)} %get-tuple-element.36.p3.refs_2_, ...), custom_call_target="tpu_custom_call" | custom-call | flops 1000000000 | tf_op jit(solution)/shard_map/pallas_call | solution.py:40
  62.5 2.8 %shard_map.84 = (bf16[1,3072,512]{2,1,0:T(8,128)(2,1)}, f32[64,512]{1,0:T(8,128)}) custom-call(s32[2]{0:T(128)S(1)} %pad_add_fusion.ids, f32[128,128]{1,0:T(8,128)S(1)} %shard_map.80.keep, f32[128,128]{1,0:T(8,128)S(1)} %collective-permute-done.21.other, f32[64,64]{1,0:T(8,128)S(1)} %shard_map.82.refs_3_.lower_inv, ...), custom_call_target="tpu_custom_call" | custom-call | flops 1000000000 | tf_op jit(solution)/shard_map/pallas_call | solution.py:40
  (35 shorter events, 5.0 us)
Async XLA Ops:
  0.7 1.6 %copy-start = (bf16[512,512]{1,0:T(8,128)(2,1)S(1)}, bf16[512,512]{1,0:T(8,128)(2,1)}, u32[]{:S(2)}) copy-start(bf16[512,512]{1,0:T(8,128)(2,1)} %yv.1) | copy-start | bytes 1572868
  0.7 1.6 %copy-start.1 = (f32[512,64]{0,1:T(8,128)S(1)}, f32[512,64]{0,1:T(8,128)}, u32[]{:S(2)}) copy-start(f32[512,64]{0,1:T(8,128)} %param.7) | copy-start | bytes 393220
  5.6 2.1 %collective-permute-start = (f32[768,128]{1,0:T(8,128)S(1)}, f32[768,128]{1,0:T(8,128)S(1)}, u32[]{:S(2)}, u32[]{:S(2)}) collective-permute-start(f32[768,128]{1,0:T(8,128)S(1)} %get-tuple-element.28), channel_id=1, source_target_pairs={{0,1},{1,0},{2,3},{3,2},{4,5},{5,4},{6,7},{7,6},{8,9},{9,8},{10,11... | collective-permute-start | bytes 1179656 | tf_op jit(solution)/shard_map/ppermute | solution.py:313
  7.8 6.0 %collective-permute-start.1 = (f32[192,128]{1,0:T(8,128)S(1)}, f32[192,128]{1,0:T(8,128)S(1)}, u32[]{:S(2)}, u32[]{:S(2)}) collective-permute-start(f32[192,128]{1,0:T(8,128)S(1)} %get-tuple-element.30), channel_id=1, source_target_pairs={{0,2},{2,0},{4,6},{6,4},{1,3},{3,1},{5,7},{7,5},{8,10},{10,8},{12,... | collective-permute-start | bytes 294920 | tf_op jit(solution)/shard_map/ppermute | solution.py:313
  10.5 5.9 %collective-permute-start.2 = (f32[192,128]{1,0:T(8,128)S(1)}, f32[192,128]{1,0:T(8,128)S(1)}, u32[]{:S(2)}, u32[]{:S(2)}) collective-permute-start(f32[192,128]{1,0:T(8,128)S(1)} %get-tuple-element.31), channel_id=1, source_target_pairs={{0,4},{2,6},{4,0},{6,2},{1,5},{3,7},{5,1},{7,3},{8,12},{10,14},{12... | collective-permute-start | bytes 294920 | tf_op jit(solution)/shard_map/ppermute | solution.py:313
  12.0 5.5 %collective-permute-start.3 = (f32[192,128]{1,0:T(8,128)S(1)}, f32[192,128]{1,0:T(8,128)S(1)}, u32[]{:S(2)}, u32[]{:S(2)}) collective-permute-start(f32[192,128]{1,0:T(8,128)S(1)} %get-tuple-element.32), channel_id=1, source_target_pairs={{0,6},{2,4},{4,2},{6,0},{1,7},{3,5},{5,3},{7,1},{8,14},{10,12},{12... | collective-permute-start | bytes 294920 | tf_op jit(solution)/shard_map/ppermute | solution.py:313
  17.6 5.5 %collective-permute-start.4 = (f32[192,128]{1,0:T(8,128)S(1)}, f32[192,128]{1,0:T(8,128)S(1)}, u32[]{:S(2)}, u32[]{:S(2)}) collective-permute-start(f32[192,128]{1,0:T(8,128)S(1)} %shard_map.71.refs_0_), channel_id=1, source_target_pairs={{0,8},{8,0},{16,24},{24,16},{1,9},{9,1},{17,25},{25,17},{2,10},{10... | collective-permute-start | bytes 294920 | tf_op jit(solution)/shard_map/ppermute | solution.py:313
  19.2 9.2 %collective-permute-start.5 = (f32[192,128]{1,0:T(8,128)S(1)}, f32[192,128]{1,0:T(8,128)S(1)}, u32[]{:S(2)}, u32[]{:S(2)}) collective-permute-start(f32[192,128]{1,0:T(8,128)S(1)} %shard_map.71.refs_0_), channel_id=1, source_target_pairs={{0,16},{8,24},{16,0},{24,8},{1,17},{9,25},{17,1},{25,9},{2,18},{10... | collective-permute-start | bytes 294920 | tf_op jit(solution)/shard_map/ppermute | solution.py:313
  21.8 6.7 %collective-permute-start.6 = (f32[192,128]{1,0:T(8,128)S(1)}, f32[192,128]{1,0:T(8,128)S(1)}, u32[]{:S(2)}, u32[]{:S(2)}) collective-permute-start(f32[192,128]{1,0:T(8,128)S(1)} %shard_map.71.refs_0_), channel_id=1, source_target_pairs={{0,24},{8,16},{16,8},{24,0},{1,25},{9,17},{17,9},{25,1},{2,26},{10... | collective-permute-start | bytes 294920 | tf_op jit(solution)/shard_map/ppermute | solution.py:313
  28.5 4.7 %collective-permute-start.9 = (f32[192,128]{1,0:T(8,128)S(1)}, f32[192,128]{1,0:T(8,128)S(1)}, u32[]{:S(2)}, u32[]{:S(2)}) collective-permute-start(f32[192,128]{1,0:T(8,128)S(1)} %shard_map.72.refs_0_), channel_id=1, source_target_pairs={{0,4},{2,6},{4,0},{6,2},{1,5},{3,7},{5,1},{7,3},{8,12},{10,14},{12... | collective-permute-start | bytes 294920 | tf_op jit(solution)/shard_map/ppermute | solution.py:313
  29.8 5.5 %collective-permute-start.11 = (f32[192,128]{1,0:T(8,128)S(1)}, f32[192,128]{1,0:T(8,128)S(1)}, u32[]{:S(2)}, u32[]{:S(2)}) collective-permute-start(f32[192,128]{1,0:T(8,128)S(1)} %shard_map.72.refs_0_), channel_id=1, source_target_pairs={{0,6},{2,4},{4,2},{6,0},{1,7},{3,5},{5,3},{7,1},{8,14},{10,12},{12... | collective-permute-start | bytes 294920 | tf_op jit(solution)/shard_map/ppermute | solution.py:313
  32.0 4.6 %collective-permute-start.7 = (f32[192,128]{1,0:T(8,128)S(1)}, f32[192,128]{1,0:T(8,128)S(1)}, u32[]{:S(2)}, u32[]{:S(2)}) collective-permute-start(f32[192,128]{1,0:T(8,128)S(1)} %shard_map.72.refs_0_), channel_id=1, source_target_pairs={{0,2},{2,0},{4,6},{6,4},{1,3},{3,1},{5,7},{7,5},{8,10},{10,8},{12,... | collective-permute-start | bytes 294920 | tf_op jit(solution)/shard_map/ppermute | solution.py:313
  32.0 7.6 %collective-permute-start.13 = (f32[192,128]{1,0:T(8,128)S(1)}, f32[192,128]{1,0:T(8,128)S(1)}, u32[]{:S(2)}, u32[]{:S(2)}) collective-permute-start(f32[192,128]{1,0:T(8,128)S(1)} %shard_map.72.refs_0_), channel_id=1, source_target_pairs={{0,1},{1,0},{2,3},{3,2},{4,5},{5,4},{6,7},{7,6},{8,9},{9,8},{10,11... | collective-permute-start | bytes 294920 | tf_op jit(solution)/shard_map/ppermute | solution.py:313
  33.2 7.9 %collective-permute-start.10 = (f32[192,128]{1,0:T(8,128)S(1)}, f32[192,128]{1,0:T(8,128)S(1)}, u32[]{:S(2)}, u32[]{:S(2)}) collective-permute-start(f32[192,128]{1,0:T(8,128)S(1)} %collective-permute-done.9.refs_2_), channel_id=1, source_target_pairs={{0,1},{1,0},{2,3},{3,2},{4,5},{5,4},{6,7},{7,6},{8,9},{9,8},{10,11... | collective-permute-start | bytes 294920 | tf_op jit(solution)/shard_map/ppermute | solution.py:313
  35.3 5.8 %collective-permute-start.12 = (f32[192,128]{1,0:T(8,128)S(1)}, f32[192,128]{1,0:T(8,128)S(1)}, u32[]{:S(2)}, u32[]{:S(2)}) collective-permute-start(f32[192,128]{1,0:T(8,128)S(1)} %collective-permute-done.11.refs_3_), channel_id=1, source_target_pairs={{0,1},{1,0},{2,3},{3,2},{4,5},{5,4},{6,7},{7,6},{8,9},{9,8},{10,11... | collective-permute-start | bytes 294920 | tf_op jit(solution)/shard_map/ppermute | solution.py:313
  36.6 4.5 %collective-permute-start.8 = (f32[192,128]{1,0:T(8,128)S(1)}, f32[192,128]{1,0:T(8,128)S(1)}, u32[]{:S(2)}, u32[]{:S(2)}) collective-permute-start(f32[192,128]{1,0:T(8,128)S(1)} %collective-permute-done.7.refs_1_), channel_id=1, source_target_pairs={{0,1},{1,0},{2,3},{3,2},{4,5},{5,4},{6,7},{7,6},{8,9},{9,8},{10,11... | collective-permute-start | bytes 294920 | tf_op jit(solution)/shard_map/ppermute | solution.py:313
  42.0 1.6 %collective-permute-start.14 = (f32[128,128]{1,0:T(8,128)S(1)}, f32[128,128]{1,0:T(8,128)S(1)}, u32[]{:S(2)}, u32[]{:S(2)}) collective-permute-start(f32[128,128]{1,0:T(8,128)S(1)} %get-tuple-element.37), channel_id=1, source_target_pairs={{0,1},{1,0},{2,3},{3,2},{4,5},{5,4},{6,7},{7,6},{8,9},{9,8},{10,11... | collective-permute-start | bytes 196616 | tf_op jit(solution)/shard_map/ppermute | solution.py:313
  43.6 4.3 %collective-permute-start.15 = (f32[128,128]{1,0:T(8,128)S(1)}, f32[128,128]{1,0:T(8,128)S(1)}, u32[]{:S(2)}, u32[]{:S(2)}) collective-permute-start(f32[128,128]{1,0:T(8,128)S(1)} %shard_map.78.refs_0_), channel_id=1, source_target_pairs={{0,2},{2,0},{4,6},{6,4},{1,3},{3,1},{5,7},{7,5},{8,10},{10,8},{12,... | collective-permute-start | bytes 196616 | tf_op jit(solution)/shard_map/ppermute | solution.py:313
  44.7 5.0 %collective-permute-start.16 = (f32[128,128]{1,0:T(8,128)S(1)}, f32[128,128]{1,0:T(8,128)S(1)}, u32[]{:S(2)}, u32[]{:S(2)}) collective-permute-start(f32[128,128]{1,0:T(8,128)S(1)} %shard_map.78.refs_0_), channel_id=1, source_target_pairs={{0,4},{2,6},{4,0},{6,2},{1,5},{3,7},{5,1},{7,3},{8,12},{10,14},{12... | collective-permute-start | bytes 196616 | tf_op jit(solution)/shard_map/ppermute | solution.py:313
  45.4 5.2 %collective-permute-start.17 = (f32[128,128]{1,0:T(8,128)S(1)}, f32[128,128]{1,0:T(8,128)S(1)}, u32[]{:S(2)}, u32[]{:S(2)}) collective-permute-start(f32[128,128]{1,0:T(8,128)S(1)} %shard_map.78.refs_0_), channel_id=1, source_target_pairs={{0,6},{2,4},{4,2},{6,0},{1,7},{3,5},{5,3},{7,1},{8,14},{10,12},{12... | collective-permute-start | bytes 196616 | tf_op jit(solution)/shard_map/ppermute | solution.py:313
  50.6 6.4 %collective-permute-start.18 = (f32[128,128]{1,0:T(8,128)S(1)}, f32[128,128]{1,0:T(8,128)S(1)}, u32[]{:S(2)}, u32[]{:S(2)}) collective-permute-start(f32[128,128]{1,0:T(8,128)S(1)} %shard_map.79.refs_0_), channel_id=1, source_target_pairs={{0,8},{8,0},{16,24},{24,16},{1,9},{9,1},{17,25},{25,17},{2,10},{10... | collective-permute-start | bytes 196616 | tf_op jit(solution)/shard_map/ppermute | solution.py:313
  52.3 6.2 %collective-permute-start.19 = (f32[128,128]{1,0:T(8,128)S(1)}, f32[128,128]{1,0:T(8,128)S(1)}, u32[]{:S(2)}, u32[]{:S(2)}) collective-permute-start(f32[128,128]{1,0:T(8,128)S(1)} %shard_map.79.refs_0_), channel_id=1, source_target_pairs={{0,16},{8,24},{16,0},{24,8},{1,17},{9,25},{17,1},{25,9},{2,18},{10... | collective-permute-start | bytes 196616 | tf_op jit(solution)/shard_map/ppermute | solution.py:313
  53.7 6.2 %collective-permute-start.20 = (f32[128,128]{1,0:T(8,128)S(1)}, f32[128,128]{1,0:T(8,128)S(1)}, u32[]{:S(2)}, u32[]{:S(2)}) collective-permute-start(f32[128,128]{1,0:T(8,128)S(1)} %shard_map.79.refs_0_), channel_id=1, source_target_pairs={{0,24},{8,16},{16,8},{24,0},{1,25},{9,17},{17,9},{25,1},{2,26},{10... | collective-permute-start | bytes 196616 | tf_op jit(solution)/shard_map/ppermute | solution.py:313
  59.9 2.6 %collective-permute-start.21 = (f32[128,128]{1,0:T(8,128)S(1)}, f32[128,128]{1,0:T(8,128)S(1)}, u32[]{:S(2)}, u32[]{:S(2)}) collective-permute-start(f32[128,128]{1,0:T(8,128)S(1)} %shard_map.80.keep), channel_id=1, source_target_pairs={{0,1},{1,0},{2,3},{3,2},{4,5},{5,4},{6,7},{7,6},{8,9},{9,8},{10,11... | collective-permute-start | bytes 196616 | tf_op jit(solution)/shard_map/ppermute | solution.py:313
